TPU v7x, 32 devices: a whole 2x2x4 slice. The times are simulated.
32 devices in a mesh: seq: 8 (over y, x, core), head: 4 (over z).
Axes of the slice: x: 2, y: 2, z: 4, core: 2. Of those that a mesh axis runs over, the one named last changes fastest.
Arguments:
- text_states: bfloat16 [2048, 4096], P('seq', 'head'), may hold values from -200 to 200
- query_weight: bfloat16 [4096, 4096], P(None, 'head'), may hold values from -0.09375 to 0.09375
- image_keys: bfloat16 [4096, 1024], P('seq', 'head'), may hold values from -12 to 12
- image_values: bfloat16 [4096, 1024], P('seq', 'head'), may hold values from -24 to 24
- output_weight: bfloat16 [4096, 4096], P('head'), may hold values from -0.09375 to 0.09375
- attn_gate: float32 [1], replicated, may hold values from 0.3 to 1.5
- frame_lengths: int32 [16], replicated, may hold values from 1 to 512, 4096 in all
- frame_limit: int32 [32], replicated, may hold values from 0 to 16
Outputs:
- gated_branch: bfloat16 [2048, 4096], P('seq', 'head')
Inputs may be any that keep to these rules, and one draw needn't show every extreme that they name: `frame_lengths`: the lengths sum to 4096.
All inputs are finite; a program needn't handle non-finite values.
Results may differ from a plain program's by a relative error of at most 0.014.
The roundings to bfloat16 on the way count: a program that leaves them out, or rounds other values in their place, can miss the bound.
Values may be sent and summed in bfloat16 or wider, within the bound.
A program may use at most 128 MiB of HBM per device.

v0:
```python
import math

import jax
import jax.numpy as jnp
from jax import lax
from jax.sharding import PartitionSpec as P

HD = 128
TBLK = 64
GROUP = 4


masked_fill = -1e30


def from_behind(block, axis, distance):
    devices = range(lax.axis_size(axis))
    route = [((i - distance) % len(devices), i) for i in devices]
    return lax.ppermute(block, axis, route)


def shards(
    text_states,
    query_weight,
    image_keys,
    image_values,
    output_weight,
    attn_gate,
    frame_lengths,
    frame_limit,
):
    text_rows = text_states.shape[0]
    video_rows = image_keys.shape[0]
    local_kv = image_keys.shape[1] // HD
    seq_index = lax.axis_index("seq")
    cycle_size = lax.axis_size("seq")
    score_scale = 1.0 / math.sqrt(HD)
    queries = jnp.dot(
        lax.all_gather(text_states, "head", axis=1, tiled=True),
        query_weight,
        preferred_element_type=jnp.float32,
    ).astype(jnp.bfloat16)
    grouped_queries = (
        queries.reshape(text_rows, local_kv, GROUP, HD)
        .transpose(1, 2, 0, 3)
        .reshape(local_kv, GROUP * text_rows, HD)
    )
    frame_ends = jnp.cumsum(frame_lengths)
    block_count = text_rows // TBLK
    my_limits = lax.dynamic_slice_in_dim(frame_limit, seq_index * block_count, block_count, 0)
    group_limits = jnp.tile(jnp.repeat(my_limits, TBLK), GROUP)

    def dense_block(running, key_block, value_block, key_frames):
        best_score, weight_sum, accumulated = running
        key_head_count = key_block.reshape(key_block.shape[0], local_kv, HD)
        value_heads = value_block.reshape(value_block.shape[0], local_kv, HD)
        scores = (
            jnp.einsum(
                "sxn,lsn->sxl", grouped_queries, key_head_count, preferred_element_type=jnp.float32
            )
            * score_scale
        )
        visible = key_frames[None, None, :] < group_limits[None, :, None]
        block_best = jnp.max(jnp.where(visible, scores, masked_fill), axis=2)
        new_best = jnp.maximum(best_score, block_best)
        weights = jnp.where(visible, jnp.exp(scores - new_best[:, :, None]), 0.0)
        factor = jnp.exp(best_score - new_best)
        weight_sum = weight_sum * factor + jnp.sum(weights, axis=2)
        mixed = jnp.einsum(
            "vus,svg->vug",
            weights.astype(jnp.bfloat16),
            value_heads,
            preferred_element_type=jnp.float32,
        )
        accumulated = accumulated * factor[:, :, None] + mixed
        return (new_best, weight_sum, accumulated)

    def attend_frames(running, key_block, value_block, first_row):
        token_positions = first_row + jnp.arange(key_block.shape[0], dtype=jnp.int32)
        key_frames = jnp.sum(
            (frame_ends[None, :] <= token_positions[:, None]).astype(jnp.int32), axis=1
        )
        return dense_block(running, key_block, value_block, key_frames)

    initial = (
        jnp.full((local_kv, GROUP * text_rows), masked_fill, jnp.float32),
        jnp.zeros((local_kv, GROUP * text_rows), jnp.float32),
        jnp.zeros((local_kv, GROUP * text_rows, HD), jnp.float32),
    )
    half_rows = video_rows // 2

    def paired_turn(turn_index, state_in):
        running, keys_up, values_up, keys_down, values_down = state_in
        source_up = (seq_index - turn_index) % cycle_size
        source_down = (seq_index + turn_index) % cycle_size
        running = attend_frames(running, keys_up, values_up, source_up * video_rows)
        running = attend_frames(
            running, keys_down, values_down, source_down * video_rows + half_rows
        )
        keys_up, values_up = from_behind((keys_up, values_up), "seq", 1)
        keys_down, values_down = from_behind((keys_down, values_down), "seq", -1)
        return (running, keys_up, values_up, keys_down, values_down)

    start_state = (
        initial,
        image_keys[:half_rows],
        image_values[:half_rows],
        image_keys[half_rows:],
        image_values[half_rows:],
    )
    running, keys_up, values_up, keys_down, values_down = lax.fori_loop(
        0, cycle_size - 1, paired_turn, start_state
    )
    running = attend_frames(running, keys_up, values_up, (seq_index + 1) % cycle_size * video_rows)
    running = attend_frames(
        running, keys_down, values_down, (seq_index - 1) % cycle_size * video_rows + half_rows
    )
    best_score, weight_sum, accumulated = running
    output_groups = (accumulated / jnp.maximum(weight_sum, 1.0)[:, :, None]).astype(jnp.bfloat16)
    attention_output = (
        output_groups.reshape(local_kv, GROUP, text_rows, HD)
        .transpose(2, 0, 1, 3)
        .reshape(text_rows, local_kv * GROUP * HD)
    )
    summed = lax.psum_scatter(
        lax.dot_general(
            output_weight,
            attention_output,
            (((0,), (1,)), ((), ())),
            preferred_element_type=jnp.float32,
        ).astype(jnp.bfloat16),
        "head",
        scatter_dimension=0,
        tiled=True,
    ).astype(jnp.float32)
    return (jnp.tanh(attn_gate[0]) * summed.T).astype(jnp.bfloat16)


def solution(mesh):
    in_specs = (
        P("seq", "head"),
        P(None, "head"),
        P("seq", "head"),
        P("seq", "head"),
        P("head", None),
        P(),
        P(),
        P(),
    )
    out_specs = P("seq", "head")
    return jax.shard_map(shards, mesh=mesh, in_specs=in_specs, out_specs=out_specs, check_vma=False)
```

profile of v0, /device:TPU:1, one launch (start us, length us, event | category | flops | bytes accessed | tf_op | source)
XLA Modules:
  0.0 185.1 jit_solution(13264895358251018407)
XLA Ops:
  6.5 0.7 all-gather.2.cloned.1.call-update
  7.4 0.7 copy.44
  8.3 0.7 dynamic_slice.3
  9.6 1.1 fusion.71
  10.8 45.7 %all-gather.2.cloned.1.call-done = bf16[256,4096]{1,0:T(8,128)(2,1)} async-done(((bf16[256,1024]{1,0:T(8,128)(2,1)}), bf16[256,4096]{1,0:T(8,128)(2,1)}) %all-gather.2.cloned.1.call-update) | async-done | bytes 2097168 | tf_op jit(solution)/shard_map/all_gather | solution.py:39
  56.5 6.3 %convolution_convert_fusion.1 = bf16[256,1024]{1,0:T(8,128)(2,1)S(1)} fusion(bf16[256,4096]{1,0:T(8,128)(2,1)} %all-gather.2.cloned.1.call-done, bf16[4096,1024]{1,0:T(8,128)(2,1)} %param.11), kind=kOutput, calls=%fused_computation.65 | convolution fusion | flops 2147745792 | bytes 11010048 | tf_op jit(solution)/shard_map/dot_general | solution.py:38
  63.3 60.3 %while.28 = (s32[]{:T(128)}, f32[2,1024]{1,0:T(2,128)S(1)}, f32[2,1024]{1,0:T(2,128)S(1)}, f32[2,1024,128]{2,1,0:T(8,128)S(1)}, bf16[256,256]{1,0:T(8,128)(2,1)S...) while((s32[]{:T(128)}, f32[2,1024]{1,0:T(2,128)S(1)}, ...), condition=%wide.region_8.9_spmd.clone, body=%wide.region_1.8_spmd.clone.sunk | while | flops 550279168 | bytes 23832240 | solution.py:111
  63.5 2.0 %collective-permute-start = (bf16[256,256]{1,0:T(8,128)(2,1)S(1)}, bf16[256,256]{1,0:T(8,128)(2,1)S(1)}, u32[]{:S(2)}, u32[]{:S(2)}) collective-permute-start(bf16[256,256]{1,0:T(8,128)(2,1)S(1)} %copy.129), channel_id=1, source_target_pairs={{28,0},{0,4},{4,8},{8,12},{12,16},{16,20},{20,24},{24,28},{29,1},{... | collective-permute-start | bytes 393224 | tf_op jit(solution)/shard_map/while/body/eval_jaxpr/ppermute | solution.py:19
  65.6 0.5 collective-permute-start.2
  66.1 1.1 collective-permute-start.3
  67.7 0.6 select_reduce_fusion.6
  68.3 0.6 select_reduce_fusion.7
  68.9 0.5 fusion.116
  69.9 1.2 fusion.118
  71.2 0.8 convolution_add_fusion.5
  72.1 1.2 collective-permute-done.3
  73.3 1.6 collective-permute-start.1
  75.0 1.6 collective-permute-start.3
  77.1 0.6 select_reduce_fusion.6
  77.7 0.6 select_reduce_fusion.7
  78.3 0.5 fusion.116
  79.3 1.2 fusion.118
  80.6 0.8 convolution_add_fusion.5
  81.9 0.8 collective-permute-start.1
  82.8 2.4 %collective-permute-start.3 = (bf16[256,256]{1,0:T(8,128)(2,1)S(1)}, bf16[256,256]{1,0:T(8,128)(2,1)S(1)}, u32[]{:S(2)}, u32[]{:S(2)}) collective-permute-start(bf16[256,256]{1,0:T(8,128)(2,1)S(1)} %copy.132), channel_id=1, source_target_pairs={{4,0},{8,4},{12,8},{16,12},{20,16},{24,20},{28,24},{0,28},{5,1},{9... | collective-permute-start | bytes 393224 | tf_op jit(solution)/shard_map/while/body/eval_jaxpr/ppermute | solution.py:19
  85.7 0.6 select_reduce_fusion.6
  86.3 0.6 select_reduce_fusion.7
  86.9 0.5 fusion.116
  87.9 1.2 fusion.118
  89.1 0.8 convolution_add_fusion.5
  90.1 0.8 collective-permute-start.1
  91.0 2.4 %collective-permute-start.3 = (bf16[256,256]{1,0:T(8,128)(2,1)S(1)}, bf16[256,256]{1,0:T(8,128)(2,1)S(1)}, u32[]{:S(2)}, u32[]{:S(2)}) collective-permute-start(bf16[256,256]{1,0:T(8,128)(2,1)S(1)} %copy.132), channel_id=1, source_target_pairs={{4,0},{8,4},{12,8},{16,12},{20,16},{24,20},{28,24},{0,28},{5,1},{9... | collective-permute-start | bytes 393224 | tf_op jit(solution)/shard_map/while/body/eval_jaxpr/ppermute | solution.py:19
  93.9 0.6 select_reduce_fusion.6
  94.5 0.6 select_reduce_fusion.7
  95.1 0.5 fusion.116
  96.1 1.2 fusion.118
  97.4 0.8 convolution_add_fusion.5
  98.4 1.3 collective-permute-start.1
  99.8 1.9 %collective-permute-start.3 = (bf16[256,256]{1,0:T(8,128)(2,1)S(1)}, bf16[256,256]{1,0:T(8,128)(2,1)S(1)}, u32[]{:S(2)}, u32[]{:S(2)}) collective-permute-start(bf16[256,256]{1,0:T(8,128)(2,1)S(1)} %copy.132), channel_id=1, source_target_pairs={{4,0},{8,4},{12,8},{16,12},{20,16},{24,20},{28,24},{0,28},{5,1},{9... | collective-permute-start | bytes 393224 | tf_op jit(solution)/shard_map/while/body/eval_jaxpr/ppermute | solution.py:19
  102.2 0.6 select_reduce_fusion.6
  102.8 0.6 select_reduce_fusion.7
  103.4 0.5 fusion.116
  104.4 1.2 fusion.118
  105.6 0.8 convolution_add_fusion.5
  106.8 1.4 collective-permute-start.1
  108.4 1.8 collective-permute-start.3
  110.6 0.6 select_reduce_fusion.6
  111.2 0.6 select_reduce_fusion.7
  111.8 0.5 fusion.116
  112.8 1.2 fusion.118
  114.1 0.8 convolution_add_fusion.5
  115.4 1.1 collective-permute-start.1
  116.6 2.1 %collective-permute-start.3 = (bf16[256,256]{1,0:T(8,128)(2,1)S(1)}, bf16[256,256]{1,0:T(8,128)(2,1)S(1)}, u32[]{:S(2)}, u32[]{:S(2)}) collective-permute-start(bf16[256,256]{1,0:T(8,128)(2,1)S(1)} %copy.132), channel_id=1, source_target_pairs={{4,0},{8,4},{12,8},{16,12},{20,16},{24,20},{28,24},{0,28},{5,1},{9... | collective-permute-start | bytes 393224 | tf_op jit(solution)/shard_map/while/body/eval_jaxpr/ppermute | solution.py:19
  119.2 0.6 select_reduce_fusion.6
  119.8 0.6 select_reduce_fusion.7
  121.4 1.2 fusion.118
  122.7 0.8 convolution_add_fusion.5
  123.6 0.6 select_reduce_fusion.2
  124.1 0.6 select_reduce_fusion.3
  125.8 1.2 fusion.41
  127.0 1.0 fusion.42
  128.2 7.1 %fusion.35 = bf16[4096,256]{0,1:T(8,128)(2,1)} fusion(bf16[256,1024]{0,1:T(8,128)(2,1)S(1)} %bitcast.115, bf16[1024,4096]{1,0:T(8,128)(2,1)} %param.14), kind=kOutput, calls=%fused_computation.51 | convolution fusion | flops 2148532224 | bytes 11010048 | tf_op jit(solution)/shard_map/dot_general | solution.py:126
  136.0 40.3 %reduce-scatter.2.cloned.1.call-done = bf16[1024,256]{0,1:T(8,128)(2,1)} async-done(((bf16[4096,256]{0,1:T(8,128)(2,1)}), bf16[1024,256]{0,1:T(8,128)(2,1)}) %reduce-scatter.2.cloned.1.call-update) | async-done | bytes 524304 | tf_op jit(solution)/shard_map/reduce_scatter | solution.py:125
  176.3 1.9 %fusion.53 = bf16[256,1024]{1,0:T(8,128)(2,1)} fusion(bf16[1024,256]{0,1:T(8,128)(2,1)} %reduce-scatter.2.cloned.1.call-done, f32[]{:T(128)} %bitcast), kind=kLoop, calls=%fused_computation.75 | loop fusion | flops 786432 | bytes 1048580 | tf_op jit(solution)/shard_map/convert_element_type | solution.py:136
  (154 shorter events, 12.3 us)
Async XLA Ops:
  6.5 50.0 %all-gather.2.cloned.1.call-start = ((), (), s32[]{:S(2)}) async-start(), calls=%async_computation.1 | async-start | bytes 2621440 | tf_op jit(solution)/shard_map/all_gather | solution.py:39
  7.3 169.1 %reduce-scatter.2.cloned.1.call-start = ((), (), s32[]{:S(2)}) async-start(), calls=%async_computation.2 | async-start | bytes 2621440 | tf_op jit(solution)/shard_map/reduce_scatter | solution.py:125
  63.5 8.5 %collective-permute-start = (bf16[256,256]{1,0:T(8,128)(2,1)S(1)}, bf16[256,256]{1,0:T(8,128)(2,1)S(1)}, u32[]{:S(2)}, u32[]{:S(2)}) collective-permute-start(bf16[256,256]{1,0:T(8,128)(2,1)S(1)} %copy.129), channel_id=1, source_target_pairs={{28,0},{0,4},{4,8},{8,12},{12,16},{16,20},{20,24},{24,28},{29,1},{... | collective-permute-start | bytes 393224 | tf_op jit(solution)/shard_map/while/body/eval_jaxpr/ppermute | solution.py:19
  65.5 6.6 %collective-permute-start.1 = (bf16[256,256]{1,0:T(8,128)(2,1)S(1)}, bf16[256,256]{1,0:T(8,128)(2,1)S(1)}, u32[]{:S(2)}, u32[]{:S(2)}) collective-permute-start(bf16[256,256]{1,0:T(8,128)(2,1)S(1)} %copy.130), channel_id=1, source_target_pairs={{28,0},{0,4},{4,8},{8,12},{12,16},{16,20},{20,24},{24,28},{29,1},{... | collective-permute-start | bytes 393224 | tf_op jit(solution)/shard_map/while/body/eval_jaxpr/ppermute | solution.py:19
  65.6 6.5 %collective-permute-start.2 = (bf16[256,256]{1,0:T(8,128)(2,1)S(1)}, bf16[256,256]{1,0:T(8,128)(2,1)S(1)}, u32[]{:S(2)}, u32[]{:S(2)}) collective-permute-start(bf16[256,256]{1,0:T(8,128)(2,1)S(1)} %copy.131), channel_id=1, source_target_pairs={{4,0},{8,4},{12,8},{16,12},{20,16},{24,20},{28,24},{0,28},{5,1},{9... | collective-permute-start | bytes 393224 | tf_op jit(solution)/shard_map/while/body/eval_jaxpr/ppermute | solution.py:19
  66.1 7.1 %collective-permute-start.3 = (bf16[256,256]{1,0:T(8,128)(2,1)S(1)}, bf16[256,256]{1,0:T(8,128)(2,1)S(1)}, u32[]{:S(2)}, u32[]{:S(2)}) collective-permute-start(bf16[256,256]{1,0:T(8,128)(2,1)S(1)} %copy.132), channel_id=1, source_target_pairs={{4,0},{8,4},{12,8},{16,12},{20,16},{24,20},{28,24},{0,28},{5,1},{9... | collective-permute-start | bytes 393224 | tf_op jit(solution)/shard_map/while/body/eval_jaxpr/ppermute | solution.py:19
  73.2 8.2 %collective-permute-start = (bf16[256,256]{1,0:T(8,128)(2,1)S(1)}, bf16[256,256]{1,0:T(8,128)(2,1)S(1)}, u32[]{:S(2)}, u32[]{:S(2)}) collective-permute-start(bf16[256,256]{1,0:T(8,128)(2,1)S(1)} %copy.129), channel_id=1, source_target_pairs={{28,0},{0,4},{4,8},{8,12},{12,16},{16,20},{20,24},{24,28},{29,1},{... | collective-permute-start | bytes 393224 | tf_op jit(solution)/shard_map/while/body/eval_jaxpr/ppermute | solution.py:19
  73.3 8.1 %collective-permute-start.1 = (bf16[256,256]{1,0:T(8,128)(2,1)S(1)}, bf16[256,256]{1,0:T(8,128)(2,1)S(1)}, u32[]{:S(2)}, u32[]{:S(2)}) collective-permute-start(bf16[256,256]{1,0:T(8,128)(2,1)S(1)} %copy.130), channel_id=1, source_target_pairs={{28,0},{0,4},{4,8},{8,12},{12,16},{16,20},{20,24},{24,28},{29,1},{... | collective-permute-start | bytes 393224 | tf_op jit(solution)/shard_map/while/body/eval_jaxpr/ppermute | solution.py:19
  75.0 6.5 %collective-permute-start.2 = (bf16[256,256]{1,0:T(8,128)(2,1)S(1)}, bf16[256,256]{1,0:T(8,128)(2,1)S(1)}, u32[]{:S(2)}, u32[]{:S(2)}) collective-permute-start(bf16[256,256]{1,0:T(8,128)(2,1)S(1)} %copy.131), channel_id=1, source_target_pairs={{4,0},{8,4},{12,8},{16,12},{20,16},{24,20},{28,24},{0,28},{5,1},{9... | collective-permute-start | bytes 393224 | tf_op jit(solution)/shard_map/while/body/eval_jaxpr/ppermute | solution.py:19
  75.0 6.8 %collective-permute-start.3 = (bf16[256,256]{1,0:T(8,128)(2,1)S(1)}, bf16[256,256]{1,0:T(8,128)(2,1)S(1)}, u32[]{:S(2)}, u32[]{:S(2)}) collective-permute-start(bf16[256,256]{1,0:T(8,128)(2,1)S(1)} %copy.132), channel_id=1, source_target_pairs={{4,0},{8,4},{12,8},{16,12},{20,16},{24,20},{28,24},{0,28},{5,1},{9... | collective-permute-start | bytes 393224 | tf_op jit(solution)/shard_map/while/body/eval_jaxpr/ppermute | solution.py:19
  81.8 8.2 %collective-permute-start = (bf16[256,256]{1,0:T(8,128)(2,1)S(1)}, bf16[256,256]{1,0:T(8,128)(2,1)S(1)}, u32[]{:S(2)}, u32[]{:S(2)}) collective-permute-start(bf16[256,256]{1,0:T(8,128)(2,1)S(1)} %copy.129), channel_id=1, source_target_pairs={{28,0},{0,4},{4,8},{8,12},{12,16},{16,20},{20,24},{24,28},{29,1},{... | collective-permute-start | bytes 393224 | tf_op jit(solution)/shard_map/while/body/eval_jaxpr/ppermute | solution.py:19
  81.9 8.1 %collective-permute-start.1 = (bf16[256,256]{1,0:T(8,128)(2,1)S(1)}, bf16[256,256]{1,0:T(8,128)(2,1)S(1)}, u32[]{:S(2)}, u32[]{:S(2)}) collective-permute-start(bf16[256,256]{1,0:T(8,128)(2,1)S(1)} %copy.130), channel_id=1, source_target_pairs={{28,0},{0,4},{4,8},{8,12},{12,16},{16,20},{20,24},{24,28},{29,1},{... | collective-permute-start | bytes 393224 | tf_op jit(solution)/shard_map/while/body/eval_jaxpr/ppermute | solution.py:19
  82.7 7.3 %collective-permute-start.2 = (bf16[256,256]{1,0:T(8,128)(2,1)S(1)}, bf16[256,256]{1,0:T(8,128)(2,1)S(1)}, u32[]{:S(2)}, u32[]{:S(2)}) collective-permute-start(bf16[256,256]{1,0:T(8,128)(2,1)S(1)} %copy.131), channel_id=1, source_target_pairs={{4,0},{8,4},{12,8},{16,12},{20,16},{24,20},{28,24},{0,28},{5,1},{9... | collective-permute-start | bytes 393224 | tf_op jit(solution)/shard_map/while/body/eval_jaxpr/ppermute | solution.py:19
  82.8 7.3 %collective-permute-start.3 = (bf16[256,256]{1,0:T(8,128)(2,1)S(1)}, bf16[256,256]{1,0:T(8,128)(2,1)S(1)}, u32[]{:S(2)}, u32[]{:S(2)}) collective-permute-start(bf16[256,256]{1,0:T(8,128)(2,1)S(1)} %copy.132), channel_id=1, source_target_pairs={{4,0},{8,4},{12,8},{16,12},{20,16},{24,20},{28,24},{0,28},{5,1},{9... | collective-permute-start | bytes 393224 | tf_op jit(solution)/shard_map/while/body/eval_jaxpr/ppermute | solution.py:19
  90.1 8.2 %collective-permute-start = (bf16[256,256]{1,0:T(8,128)(2,1)S(1)}, bf16[256,256]{1,0:T(8,128)(2,1)S(1)}, u32[]{:S(2)}, u32[]{:S(2)}) collective-permute-start(bf16[256,256]{1,0:T(8,128)(2,1)S(1)} %copy.129), channel_id=1, source_target_pairs={{28,0},{0,4},{4,8},{8,12},{12,16},{16,20},{20,24},{24,28},{29,1},{... | collective-permute-start | bytes 393224 | tf_op jit(solution)/shard_map/while/body/eval_jaxpr/ppermute | solution.py:19
  90.1 8.1 %collective-permute-start.1 = (bf16[256,256]{1,0:T(8,128)(2,1)S(1)}, bf16[256,256]{1,0:T(8,128)(2,1)S(1)}, u32[]{:S(2)}, u32[]{:S(2)}) collective-permute-start(bf16[256,256]{1,0:T(8,128)(2,1)S(1)} %copy.130), channel_id=1, source_target_pairs={{28,0},{0,4},{4,8},{8,12},{12,16},{16,20},{20,24},{24,28},{29,1},{... | collective-permute-start | bytes 393224 | tf_op jit(solution)/shard_map/while/body/eval_jaxpr/ppermute | solution.py:19
  91.0 7.3 %collective-permute-start.2 = (bf16[256,256]{1,0:T(8,128)(2,1)S(1)}, bf16[256,256]{1,0:T(8,128)(2,1)S(1)}, u32[]{:S(2)}, u32[]{:S(2)}) collective-permute-start(bf16[256,256]{1,0:T(8,128)(2,1)S(1)} %copy.131), channel_id=1, source_target_pairs={{4,0},{8,4},{12,8},{16,12},{20,16},{24,20},{28,24},{0,28},{5,1},{9... | collective-permute-start | bytes 393224 | tf_op jit(solution)/shard_map/while/body/eval_jaxpr/ppermute | solution.py:19
  91.0 7.3 %collective-permute-start.3 = (bf16[256,256]{1,0:T(8,128)(2,1)S(1)}, bf16[256,256]{1,0:T(8,128)(2,1)S(1)}, u32[]{:S(2)}, u32[]{:S(2)}) collective-permute-start(bf16[256,256]{1,0:T(8,128)(2,1)S(1)} %copy.132), channel_id=1, source_target_pairs={{4,0},{8,4},{12,8},{16,12},{20,16},{24,20},{28,24},{0,28},{5,1},{9... | collective-permute-start | bytes 393224 | tf_op jit(solution)/shard_map/while/body/eval_jaxpr/ppermute | solution.py:19
  98.3 8.2 %collective-permute-start = (bf16[256,256]{1,0:T(8,128)(2,1)S(1)}, bf16[256,256]{1,0:T(8,128)(2,1)S(1)}, u32[]{:S(2)}, u32[]{:S(2)}) collective-permute-start(bf16[256,256]{1,0:T(8,128)(2,1)S(1)} %copy.129), channel_id=1, source_target_pairs={{28,0},{0,4},{4,8},{8,12},{12,16},{16,20},{20,24},{24,28},{29,1},{... | collective-permute-start | bytes 393224 | tf_op jit(solution)/shard_map/while/body/eval_jaxpr/ppermute | solution.py:19
  98.4 8.1 %collective-permute-start.1 = (bf16[256,256]{1,0:T(8,128)(2,1)S(1)}, bf16[256,256]{1,0:T(8,128)(2,1)S(1)}, u32[]{:S(2)}, u32[]{:S(2)}) collective-permute-start(bf16[256,256]{1,0:T(8,128)(2,1)S(1)} %copy.130), channel_id=1, source_target_pairs={{28,0},{0,4},{4,8},{8,12},{12,16},{16,20},{20,24},{24,28},{29,1},{... | collective-permute-start | bytes 393224 | tf_op jit(solution)/shard_map/while/body/eval_jaxpr/ppermute | solution.py:19
  99.7 6.8 %collective-permute-start.2 = (bf16[256,256]{1,0:T(8,128)(2,1)S(1)}, bf16[256,256]{1,0:T(8,128)(2,1)S(1)}, u32[]{:S(2)}, u32[]{:S(2)}) collective-permute-start(bf16[256,256]{1,0:T(8,128)(2,1)S(1)} %copy.131), channel_id=1, source_target_pairs={{4,0},{8,4},{12,8},{16,12},{20,16},{24,20},{28,24},{0,28},{5,1},{9... | collective-permute-start | bytes 393224 | tf_op jit(solution)/shard_map/while/body/eval_jaxpr/ppermute | solution.py:19
  99.8 6.9 %collective-permute-start.3 = (bf16[256,256]{1,0:T(8,128)(2,1)S(1)}, bf16[256,256]{1,0:T(8,128)(2,1)S(1)}, u32[]{:S(2)}, u32[]{:S(2)}) collective-permute-start(bf16[256,256]{1,0:T(8,128)(2,1)S(1)} %copy.132), channel_id=1, source_target_pairs={{4,0},{8,4},{12,8},{16,12},{20,16},{24,20},{28,24},{0,28},{5,1},{9... | collective-permute-start | bytes 393224 | tf_op jit(solution)/shard_map/while/body/eval_jaxpr/ppermute | solution.py:19
  106.8 8.2 %collective-permute-start = (bf16[256,256]{1,0:T(8,128)(2,1)S(1)}, bf16[256,256]{1,0:T(8,128)(2,1)S(1)}, u32[]{:S(2)}, u32[]{:S(2)}) collective-permute-start(bf16[256,256]{1,0:T(8,128)(2,1)S(1)} %copy.129), channel_id=1, source_target_pairs={{28,0},{0,4},{4,8},{8,12},{12,16},{16,20},{20,24},{24,28},{29,1},{... | collective-permute-start | bytes 393224 | tf_op jit(solution)/shard_map/while/body/eval_jaxpr/ppermute | solution.py:19
  106.8 8.1 %collective-permute-start.1 = (bf16[256,256]{1,0:T(8,128)(2,1)S(1)}, bf16[256,256]{1,0:T(8,128)(2,1)S(1)}, u32[]{:S(2)}, u32[]{:S(2)}) collective-permute-start(bf16[256,256]{1,0:T(8,128)(2,1)S(1)} %copy.130), channel_id=1, source_target_pairs={{28,0},{0,4},{4,8},{8,12},{12,16},{16,20},{20,24},{24,28},{29,1},{... | collective-permute-start | bytes 393224 | tf_op jit(solution)/shard_map/while/body/eval_jaxpr/ppermute | solution.py:19
  108.3 6.7 %collective-permute-start.2 = (bf16[256,256]{1,0:T(8,128)(2,1)S(1)}, bf16[256,256]{1,0:T(8,128)(2,1)S(1)}, u32[]{:S(2)}, u32[]{:S(2)}) collective-permute-start(bf16[256,256]{1,0:T(8,128)(2,1)S(1)} %copy.131), channel_id=1, source_target_pairs={{4,0},{8,4},{12,8},{16,12},{20,16},{24,20},{28,24},{0,28},{5,1},{9... | collective-permute-start | bytes 393224 | tf_op jit(solution)/shard_map/while/body/eval_jaxpr/ppermute | solution.py:19
  108.4 6.9 %collective-permute-start.3 = (bf16[256,256]{1,0:T(8,128)(2,1)S(1)}, bf16[256,256]{1,0:T(8,128)(2,1)S(1)}, u32[]{:S(2)}, u32[]{:S(2)}) collective-permute-start(bf16[256,256]{1,0:T(8,128)(2,1)S(1)} %copy.132), channel_id=1, source_target_pairs={{4,0},{8,4},{12,8},{16,12},{20,16},{24,20},{28,24},{0,28},{5,1},{9... | collective-permute-start | bytes 393224 | tf_op jit(solution)/shard_map/while/body/eval_jaxpr/ppermute | solution.py:19
  115.3 8.2 %collective-permute-start = (bf16[256,256]{1,0:T(8,128)(2,1)S(1)}, bf16[256,256]{1,0:T(8,128)(2,1)S(1)}, u32[]{:S(2)}, u32[]{:S(2)}) collective-permute-start(bf16[256,256]{1,0:T(8,128)(2,1)S(1)} %copy.129), channel_id=1, source_target_pairs={{28,0},{0,4},{4,8},{8,12},{12,16},{16,20},{20,24},{24,28},{29,1},{... | collective-permute-start | bytes 393224 | tf_op jit(solution)/shard_map/while/body/eval_jaxpr/ppermute | solution.py:19
  115.4 8.1 %collective-permute-start.1 = (bf16[256,256]{1,0:T(8,128)(2,1)S(1)}, bf16[256,256]{1,0:T(8,128)(2,1)S(1)}, u32[]{:S(2)}, u32[]{:S(2)}) collective-permute-start(bf16[256,256]{1,0:T(8,128)(2,1)S(1)} %copy.130), channel_id=1, source_target_pairs={{28,0},{0,4},{4,8},{8,12},{12,16},{16,20},{20,24},{24,28},{29,1},{... | collective-permute-start | bytes 393224 | tf_op jit(solution)/shard_map/while/body/eval_jaxpr/ppermute | solution.py:19
  116.6 7.0 %collective-permute-start.2 = (bf16[256,256]{1,0:T(8,128)(2,1)S(1)}, bf16[256,256]{1,0:T(8,128)(2,1)S(1)}, u32[]{:S(2)}, u32[]{:S(2)}) collective-permute-start(bf16[256,256]{1,0:T(8,128)(2,1)S(1)} %copy.131), channel_id=1, source_target_pairs={{4,0},{8,4},{12,8},{16,12},{20,16},{24,20},{28,24},{0,28},{5,1},{9... | collective-permute-start | bytes 393224 | tf_op jit(solution)/shard_map/while/body/eval_jaxpr/ppermute | solution.py:19
  116.6 6.9 %collective-permute-start.3 = (bf16[256,256]{1,0:T(8,128)(2,1)S(1)}, bf16[256,256]{1,0:T(8,128)(2,1)S(1)}, u32[]{:S(2)}, u32[]{:S(2)}) collective-permute-start(bf16[256,256]{1,0:T(8,128)(2,1)S(1)} %copy.132), channel_id=1, source_target_pairs={{4,0},{8,4},{12,8},{16,12},{20,16},{24,20},{28,24},{0,28},{5,1},{9... | collective-permute-start | bytes 393224 | tf_op jit(solution)/shard_map/while/body/eval_jaxpr/ppermute | solution.py:19
Sparse Core Ops, SparseCore 0:
  8.9 47.5 all-gather.1
  135.5 40.8 reduce-scatter.1
where the time goes:
time: 186 us; the launch traced here: 185 us
  waiting for transfers between devices  89 us (48%)
  matrix products  39.2 us (21%)
  starting transfers between devices  23.8 us (13%)
  other arithmetic  14.2 us (8%)
  between operations  14.2 us (8%)
  local copies, waits for them, and re-layouts  3.77 us (2%)
    all_gather x1, waiting for transfers between devices, shards(): lax.all_gather(text_states, 'head', axis=1, tiled=True)  45.7 us
    reduce_scatter x1, waiting for transfers between devices, shards(): lax.psum_scatter(lax.dot_general(output_weight, attention_output, (((0,),...  40.3 us
    ppermute x28, starting transfers between devices, from_behind(): return lax.ppermute(block, axis, route)  23.7 us
    dot_general x16, matrix products, dense_block(): jnp.einsum('vus,svg->vug', weights.astype(jnp.bfloat16), value_heads, pre...  16.7 us
    dot_general x16, matrix products, dense_block(): jnp.einsum('sxn,lsn->sxl', grouped_queries, key_head_count, preferred_ele...  9.04 us
    reduce_sum x16, other arithmetic, dense_block(): weight_sum = weight_sum * factor + jnp.sum(weights, axis=2)  8.05 us
    dot_general x1, matrix products, shards(): lax.dot_general(output_weight, attention_output, (((0,), (1,)), ((), ()))...  7.11 us
    dot_general x1, matrix products, shards(): jnp.dot(lax.all_gather(text_states, 'head', axis=1, tiled=True), query_we...  6.34 us
  transfers between devices with their start and end apart: 30, of which 6 were waited for; matrix products, arithmetic and copies ran while one was open for 20% of the time, Pallas kernels for 0%

commit v1 on v0

v1 whole, which is shorter than its diff:
```python
import functools
import math

import jax
import jax.numpy as jnp
from jax import lax
from jax.experimental import pallas as pl
from jax.experimental.pallas import tpu as pltpu
from jax.sharding import PartitionSpec as P

HD = 128
TBLK = 64
GROUP = 4
SUPER = 4096
LOW = -1e30


def kernel(
    n, p, text, wq_hbm, k_hbm, v_hbm, wo_hbm, gate, lengths, limits, out,
    tbuf, wq, wo, kbuf, vbuf, qbuf, abuf, scores, pbuf, sbuf, rup, rdn,
    local_sem, t_recv, t_up, t_dn, r_up, r_dn, r_send, k_recv, k_send, v_recv, v_send,
):
    s = lax.axis_index("seq")
    z = lax.axis_index("head")
    rows, feat = text.shape
    chunks = rows // TBLK
    vid = k_hbm.shape[0]
    local_kv = k_hbm.shape[1] // HD
    bits = n.bit_length() - 1

    def flip(index, mask):
        for b in range(bits):
            bit = 1 << b
            if mask & bit:
                index = index + bit - 2 * bit * ((index // bit) % 2)
        return index

    key_order = [*range(1, bits), 0]
    value_order = [*range(2, bits), 1, 0] if bits > 1 else [0]

    barrier = pltpu.get_barrier_semaphore()
    has_up, has_dn = z < p - 1, z > 0
    for b in range(bits):
        pl.semaphore_signal(barrier, inc=1, device_id={"seq": flip(s, 1 << b)})

    @pl.when(has_up)
    def _():
        pl.semaphore_signal(barrier, inc=1, device_id={"head": z + 1})

    @pl.when(has_dn)
    def _():
        pl.semaphore_signal(barrier, inc=1, device_id={"head": z - 1})

    local = [
        pltpu.make_async_copy(text, tbuf.at[z], local_sem.at[0]),
        pltpu.make_async_copy(wq_hbm, wq, local_sem.at[1]),
        pltpu.make_async_copy(k_hbm, kbuf.at[s], local_sem.at[2]),
        pltpu.make_async_copy(v_hbm, vbuf.at[s], local_sem.at[3]),
        pltpu.make_async_copy(wo_hbm, wo, local_sem.at[4]),
    ]
    for copy in local:
        copy.start()
    peers = bits + jnp.where(has_up, 1, 0) + jnp.where(has_dn, 1, 0)
    pl.semaphore_wait(barrier, peers)

    def span(c):
        return pl.ds(pl.multiple_of(c * TBLK, TBLK), TBLK)

    def text_copy(c, source, up, own=False):
        block = tbuf.at[source, span(c)]
        return pltpu.make_async_remote_copy(
            src_ref=text.at[span(c)] if own else block,
            dst_ref=block,
            send_sem=(t_up if up else t_dn).at[c * p + source],
            recv_sem=t_recv.at[c * p + source],
            device_id={"head": z + 1 if up else z - 1},
        )

    def text_own(c):
        @pl.when(has_up)
        def _():
            text_copy(c, z, True, True).start()

        @pl.when(has_dn)
        def _():
            text_copy(c, z, False, True).start()

    def text_hop(c, d):
        @pl.when(z - d >= 0)
        def _():
            text_copy(c, z - d, True).wait_recv()

            @pl.when(has_up)
            def _():
                text_copy(c, z - d, True).start()

        @pl.when(z + d < p)
        def _():
            text_copy(c, z + d, False).wait_recv()

            @pl.when(has_dn)
            def _():
                text_copy(c, z + d, False).start()

    def kv_copy(keys, mask, b):
        buf, hbm = (kbuf, k_hbm) if keys else (vbuf, v_hbm)
        recv, send = (k_recv, k_send) if keys else (v_recv, v_send)
        block = buf.at[flip(s, mask)]
        return pltpu.make_async_remote_copy(
            src_ref=hbm if mask == 0 else block,
            dst_ref=block,
            send_sem=send.at[mask | (1 << b)],
            recv_sem=recv.at[mask | (1 << b)],
            device_id={"seq": flip(s, 1 << b)},
        )

    def kv_send(keys, mask, step):
        order = key_order if keys else value_order
        for b in order[step:]:
            kv_copy(keys, mask, b).start()

    def kv_wait(keys, mask):
        buf, recv, send = (kbuf, k_recv, k_send) if keys else (vbuf, v_recv, v_send)
        block = buf.at[flip(s, mask)]
        pltpu.make_async_remote_copy(
            src_ref=block, dst_ref=block, send_sem=send.at[mask], recv_sem=recv.at[mask],
            device_id={"seq": flip(s, 1)},
        ).wait_recv()

    def masks_before(order, step):
        masks = [0]
        for b in order[:step]:
            masks = masks + [m | (1 << b) for m in masks]
        return masks

    def kv_step(step):
        for m_index in range(1 << step):
            for keys, order in ((True, key_order), (False, value_order)):
                mask = masks_before(order, step)[m_index] | (1 << order[step])
                kv_wait(keys, mask)
                kv_send(keys, mask, step + 1)

    def sum_copy(c, d, up):
        return pltpu.make_async_remote_copy(
            src_ref=sbuf.at[c * p + d],
            dst_ref=(rup if up else rdn).at[c * p + d],
            send_sem=r_send.at[c * p + d],
            recv_sem=(r_up if up else r_dn).at[c * p + d],
            device_id={"head": z + 1 if up else z - 1},
        )

    def sum_hop(c, h):
        for d in reversed(range(p)):
            @pl.when((z == h) & (z < d))
            def _():
                sum_copy(c, d, True).wait_recv()
                i = c * p + d
                sbuf[i] = (pbuf[i] + rup[i].astype(jnp.float32)).astype(jnp.bfloat16)
                sum_copy(c, d, True).start()
        for d in range(p):
            @pl.when((p - 1 - z == h) & (d < z))
            def _():
                sum_copy(c, d, False).wait_recv()
                i = c * p + d
                sbuf[i] = (pbuf[i] + rdn[i].astype(jnp.float32)).astype(jnp.bfloat16)
                sum_copy(c, d, False).start()

    def sum_last(c):
        i = c * p + z

        @pl.when(has_dn)
        def _():
            sum_copy(c, z, True).wait_recv()
            pbuf[i] = pbuf[i] + rup[i].astype(jnp.float32)

        @pl.when(has_up)
        def _():
            sum_copy(c, z, False).wait_recv()
            pbuf[i] = pbuf[i] + rdn[i].astype(jnp.float32)

        factor = jnp.tanh(jnp.full((1, out.shape[1]), gate[0], jnp.float32))
        out[span(c), :] = (factor * pbuf[i]).astype(jnp.bfloat16)

    def project(c):
        wide = 256

        def tile(j, carry):
            cols = pl.ds(pl.multiple_of(j * wide, wide), wide)
            total = jnp.zeros((TBLK, wide), jnp.float32)
            for source in range(p):
                total += jnp.dot(
                    tbuf[source, span(c), :], wq[source * feat : (source + 1) * feat, cols],
                    preferred_element_type=jnp.float32,
                )
            qbuf[:, cols] = total.astype(jnp.bfloat16)
            return carry

        lax.fori_loop(0, qbuf.shape[1] // wide, tile, 0)

    per = min(n, max(1, SUPER // vid))
    score_scale = math.log2(math.e) / math.sqrt(HD)

    def head_cols(h):
        return pl.ds(pl.multiple_of(h * HD, HD), HD)

    def visible_tokens(c):
        limit = limits[s * chunks + c]
        total = jnp.int32(0)
        for f in range(lengths.shape[0]):
            total += jnp.where(f < limit, lengths[f], 0)
        return total

    def attend(c, h, seen):
        q = jnp.concatenate([qbuf[:, head_cols(h * GROUP + g)] for g in range(GROUP)], axis=0)
        m_rows = GROUP * TBLK

        def lanes(x, op):
            parts = [x[:, i * HD : (i + 1) * HD] for i in range(x.shape[1] // HD)]
            return functools.reduce(op, parts)

        def part(u, state):
            best, weight, acc = state
            wide = jnp.full((m_rows, HD), LOW, jnp.float32)
            for i in range(per):
                block = u * per + i
                x = lax.dot_general(
                    q, kbuf[block, :, head_cols(h)], (((1,), (1,)), ((), ())),
                    preferred_element_type=jnp.float32,
                ) * score_scale
                column = block * vid + lax.broadcasted_iota(jnp.int32, (1, vid), 1)
                x = jnp.where(column < seen, x, LOW)
                scores[:, i * vid : (i + 1) * vid] = x
                wide = jnp.maximum(wide, lanes(x, jnp.maximum))
            new_best = jnp.maximum(best, jnp.max(wide, axis=1, keepdims=True))
            factor = jnp.exp2(best - new_best)
            weight, acc = weight * factor, acc * factor
            for i in range(per):
                w = jnp.exp2(scores[:, i * vid : (i + 1) * vid] - new_best)
                weight = weight + lanes(w, jnp.add)
                acc = acc + jnp.dot(
                    w.astype(jnp.bfloat16), vbuf[u * per + i, :, head_cols(h)],
                    preferred_element_type=jnp.float32,
                )
            return new_best, weight, acc

        state = (
            jnp.full((m_rows, 1), LOW, jnp.float32),
            jnp.zeros((m_rows, HD), jnp.float32),
            jnp.zeros((m_rows, HD), jnp.float32),
        )
        if n // per == 1:
            state = part(0, state)
        else:
            state = lax.fori_loop(0, n // per, part, state)
        _, weight, acc = state
        total = jnp.maximum(jnp.sum(weight, axis=1, keepdims=True), 1.0)
        result = jnp.where(seen > 0, acc / total, 0.0).astype(jnp.bfloat16)
        for g in range(GROUP):
            abuf[:, head_cols(h * GROUP + g)] = result[g * TBLK : (g + 1) * TBLK]

    def combine(c):
        wide = 512
        out_cols = pbuf.shape[2]

        def dest(j, carry):
            d = jnp.where(z < p // 2, p - 1 - j, j)

            def tile(t, carry):
                cols = pl.ds(pl.multiple_of(d * out_cols + t * wide, wide), wide)
                pbuf[c * p + d, :, pl.ds(pl.multiple_of(t * wide, wide), wide)] = jnp.dot(
                    abuf[...], wo[:, cols], preferred_element_type=jnp.float32
                )
                return carry

            lax.fori_loop(0, out_cols // wide, tile, 0)

            @pl.when((z == 0) & (d > 0))
            def _():
                sbuf[c * p + d] = pbuf[c * p + d].astype(jnp.bfloat16)
                sum_copy(c, d, True).start()

            @pl.when((z == p - 1) & (d < z))
            def _():
                sbuf[c * p + d] = pbuf[c * p + d].astype(jnp.bfloat16)
                sum_copy(c, d, False).start()

            return carry

        lax.fori_loop(0, p, dest, 0)

    def guarded(ok, f, *args):
        if isinstance(ok, bool):
            if ok:
                f(*args)
        else:
            pl.when(ok)(lambda: f(*args))

    text_own(0)
    kv_send(True, 0, 0)
    kv_send(False, 0, 0)
    for c in range(1, p):
        for h in range(c - 1, 0, -1):
            if c - 1 - h < chunks:
                text_hop(c - 1 - h, h)
        if c < min(chunks, p - 1):
            text_own(c)
        if c == min(2, p - 1) and bits:
            kv_step(0)

    def step(c, carry):
        @pl.when(c == 0)
        def _():
            local[0].wait()
            local[1].wait()

        text_hop(c, p - 1)
        project(c)
        for h in range(p - 2, 0, -1):
            guarded(c + p - 1 - h < chunks, text_hop, c + p - 1 - h, h)
        guarded(c + p - 1 < chunks, text_own, c + p - 1)

        @pl.when(c == 0)
        def _():
            for k in range(1, bits):
                kv_step(k)
            for copy in local[2:]:
                copy.wait()

        seen = visible_tokens(c)

        def head(h, carry):
            attend(c, h, seen)
            return carry

        lax.fori_loop(0, local_kv, head, 0)
        guarded(c - p + 1 >= 0, sum_last, c - p + 1)
        for h in range(p - 2, 0, -1):
            guarded(c - h >= 0, sum_hop, c - h, h)
        combine(c)
        return carry

    lax.fori_loop(0, chunks, step, 0)
    for k in range(p - 1):
        c = chunks + k
        for h in range(p - 1, 0, -1):
            if 0 <= c - h < chunks:
                sum_last(c - h) if h == p - 1 else sum_hop(c - h, h)

    for keys, order in ((True, key_order), (False, value_order)):
        for step_no in range(bits):
            for mask in masks_before(order, step_no):
                kv_copy(keys, mask, order[step_no]).wait_send()

    def drain(c, carry):
        for d in range(p):
            @pl.when((d <= z) & has_up)
            def _():
                text_copy(c, d, True).wait_send()

            @pl.when((d >= z) & has_dn)
            def _():
                text_copy(c, d, False).wait_send()

            @pl.when(d != z)
            def _():
                sum_copy(c, d, True).wait_send()
        return carry

    lax.fori_loop(0, chunks, drain, 0)


def solution(mesh):
    n, p = mesh.shape["seq"], mesh.shape["head"]

    def shards(text, wq, keys, values, wo, gate, lengths, limits):
        rows, feat = text.shape
        vid = keys.shape[0]
        chunks = rows // TBLK
        q_cols = wq.shape[1]
        out_cols = wo.shape[1] // p
        dma = pltpu.SemaphoreType.DMA
        any_spec = pl.BlockSpec(memory_space=pl.ANY)
        smem = pl.BlockSpec(memory_space=pltpu.SMEM)
        bf16, f32 = jnp.bfloat16, jnp.float32
        return pl.pallas_call(
            functools.partial(kernel, n, p),
            out_shape=jax.ShapeDtypeStruct((rows, out_cols), bf16),
            in_specs=[any_spec] * 5 + [smem] * 3,
            out_specs=pl.BlockSpec(memory_space=pltpu.VMEM),
            scratch_shapes=[
                pltpu.VMEM((p, rows, feat), bf16),
                pltpu.VMEM(wq.shape, bf16),
                pltpu.VMEM(wo.shape, bf16),
                pltpu.VMEM((n,) + keys.shape, bf16),
                pltpu.VMEM((n,) + values.shape, bf16),
                pltpu.VMEM((TBLK, q_cols), bf16),
                pltpu.VMEM((TBLK, q_cols), bf16),
                pltpu.VMEM((GROUP * TBLK, min(n * vid, max(vid, SUPER))), f32),
                pltpu.VMEM((chunks * p, TBLK, out_cols), f32),
                pltpu.VMEM((chunks * p, TBLK, out_cols), bf16),
                pltpu.VMEM((chunks * p, TBLK, out_cols), bf16),
                pltpu.VMEM((chunks * p, TBLK, out_cols), bf16),
                dma((5,)),
                dma((chunks * p,)), dma((chunks * p,)), dma((chunks * p,)),
                dma((chunks * p,)), dma((chunks * p,)), dma((chunks * p,)),
                dma((n,)), dma((n,)), dma((n,)), dma((n,)),
            ],
            compiler_params=pltpu.CompilerParams(
                collective_id=0, has_side_effects=True, vmem_limit_bytes=67043328
            ),
        )(text, wq, keys, values, wo, gate, lengths, limits)

    in_specs = (
        P("seq", "head"), P(None, "head"), P("seq", "head"), P("seq", "head"),
        P("head", None), P(), P(), P(),
    )
    return jax.shard_map(
        shards, mesh=mesh, in_specs=in_specs, out_specs=P("seq", "head"), check_vma=False
    )
```

time: 186 us -> 78.1 us (0.42)
  waiting for transfers between devices: 89 us -> 0 us
  Pallas kernels: 0 us -> 75.4 us
  matrix products: 39.2 us -> 0 us
  starting transfers between devices: 23.8 us -> 0 us
  other arithmetic: 14.2 us -> 0 us
  between operations: 14.2 us -> 0.66 us
  local copies, waits for them, and re-layouts: 3.77 us -> 1.87 us
    pallas_call x0 -> x1, Pallas kernels: none -> 75.4 us  [shards(): pl.pallas_call(functools.partial(kernel, n, p), out_shape=jax.ShapeDtypeS...]
    all_gather x1 -> x0, waiting for transfers between devices: 45.7 us -> none  [shards(): lax.all_gather(text_states, 'head', axis=1, tiled=True)]
    reduce_scatter x1 -> x0, waiting for transfers between devices: 40.3 us -> none  [shards(): lax.psum_scatter(lax.dot_general(output_weight, attention_output, (((0,),...]
    dot_general x34 -> x0, matrix products: 39.2 us -> none  [the longest x16 16.7 us: dense_block(): jnp.einsum('vus,svg->vug', weights.astype(jnp.bfloat16), value_heads, pre...]
    ppermute x28 -> x0, starting transfers between devices: 23.7 us -> none  [from_behind(): return lax.ppermute(block, axis, route)]
    reduce_sum x24 -> x0, other arithmetic: 8.77 us -> none  [the longest x16 8.05 us: dense_block(): weight_sum = weight_sum * factor + jnp.sum(weights, axis=2)]
    lt x8 -> x0, other arithmetic: 2.89 us -> none  [dense_block(): visible = key_frames[None, None, :] < group_limits[None, :, None]]
    ppermute x28 -> x0, waiting for transfers between devices: 2.24 us -> none  [from_behind(): return lax.ppermute(block, axis, route)]
  transfers between devices with their start and end apart: 30 -> 0, of which waited for: 6 -> 0; matrix products, arithmetic and copies ran while one was open for 20% -> 0% of each run, Pallas kernels for 0% -> 0%
where the time goes in v1:
time: 78.1 us; the launch traced here: 78 us
  Pallas kernels  75.4 us (97%)
  local copies, waits for them, and re-layouts  1.87 us (2%)
    pallas_call x1, Pallas kernels, shards(): pl.pallas_call(functools.partial(kernel, n, p), out_shape=jax.ShapeDtypeS...  75.4 us
    unnamed x1, local copies, waits for them, and re-layouts  1.87 us

profile of v1, /device:TPU:1, one launch (start us, length us, event | category | flops | bytes accessed | tf_op | source)
XLA Modules:
  0.0 78.0 jit_solution(10286267785970472255)
XLA Ops:
  0.7 75.4 %shard_map.82 = bf16[256,1024]{1,0:T(8,128)(2,1)} custom-call(bf16[256,1024]{1,0:T(8,128)(2,1)} %text.1, bf16[4096,1024]{1,0:T(8,128)(2,1)} %wq_hbm.1, bf16[512,256]{1,0:T(8,128)(2,1)} %k_hbm.1, bf16[512,256]{1,0:T(8,128)(2,1)} %v_hbm.1, bf16[1024,4096]{1,0:T(8,128)(2,1)} %wo_hbm.1, f32[1]{0:T(128)S(6)} %copy.10.gate, s32[16]{0:T(128)} %lengths.1, s32[32]{0:T(128)} %limits.1), custom_call_target="tpu_custom_call" | custom-call | tf_op jit(solution)/shard_map/pallas_call | solution.py:385
  76.1 1.9 %copy.11 = bf16[256,1024]{1,0:T(8,128)(2,1)} copy(bf16[256,1024]{1,0:T(8,128)(2,1)} %shard_map.82) | data formatting | bytes 1048576

commit v2 on v1

--- a/solution.py
+++ b/solution.py
@@ -200,9 +200,6 @@
     per = min(n, max(1, SUPER // vid))
     score_scale = math.log2(math.e) / math.sqrt(HD)
 
-    def head_cols(h):
-        return pl.ds(pl.multiple_of(h * HD, HD), HD)
-
     def visible_tokens(c):
         limit = limits[s * chunks + c]
         total = jnp.int32(0)
@@ -210,53 +207,69 @@
             total += jnp.where(f < limit, lengths[f], 0)
         return total
 
-    def attend(c, h, seen):
-        q = jnp.concatenate([qbuf[:, head_cols(h * GROUP + g)] for g in range(GROUP)], axis=0)
+    def attend(seen):
         m_rows = GROUP * TBLK
 
         def lanes(x, op):
             parts = [x[:, i * HD : (i + 1) * HD] for i in range(x.shape[1] // HD)]
             return functools.reduce(op, parts)
 
-        def part(u, state):
-            best, weight, acc = state
-            wide = jnp.full((m_rows, HD), LOW, jnp.float32)
+        def score(h, block, i, wide):
+            q = jnp.concatenate(
+                [qbuf[:, (h * GROUP + g) * HD : (h * GROUP + g + 1) * HD] for g in range(GROUP)],
+                axis=0,
+            )
+            x = lax.dot_general(
+                q, kbuf[block, :, h * HD : (h + 1) * HD], (((1,), (1,)), ((), ())),
+                preferred_element_type=jnp.float32,
+            ) * score_scale
+            column = block * vid + lax.broadcasted_iota(jnp.int32, (1, vid), 1)
+            x = jnp.where(column < seen, x, LOW)
+            scores[h % 2, :, i * vid : (i + 1) * vid] = x
+            return jnp.maximum(wide, lanes(x, jnp.maximum))
+
+        def part(u, states):
+            low = jnp.full((m_rows, HD), LOW, jnp.float32)
+            wide = low
             for i in range(per):
-                block = u * per + i
-                x = lax.dot_general(
-                    q, kbuf[block, :, head_cols(h)], (((1,), (1,)), ((), ())),
-                    preferred_element_type=jnp.float32,
-                ) * score_scale
-                column = block * vid + lax.broadcasted_iota(jnp.int32, (1, vid), 1)
-                x = jnp.where(column < seen, x, LOW)
-                scores[:, i * vid : (i + 1) * vid] = x
-                wide = jnp.maximum(wide, lanes(x, jnp.maximum))
-            new_best = jnp.maximum(best, jnp.max(wide, axis=1, keepdims=True))
-            factor = jnp.exp2(best - new_best)
-            weight, acc = weight * factor, acc * factor
-            for i in range(per):
-                w = jnp.exp2(scores[:, i * vid : (i + 1) * vid] - new_best)
-                weight = weight + lanes(w, jnp.add)
-                acc = acc + jnp.dot(
-                    w.astype(jnp.bfloat16), vbuf[u * per + i, :, head_cols(h)],
-                    preferred_element_type=jnp.float32,
-                )
-            return new_best, weight, acc
-
-        state = (
-            jnp.full((m_rows, 1), LOW, jnp.float32),
-            jnp.zeros((m_rows, HD), jnp.float32),
-            jnp.zeros((m_rows, HD), jnp.float32),
-        )
+                wide = score(0, u * per + i, i, wide)
+            done = []
+            for h in range(local_kv):
+                best, weight, acc = states[h]
+                new_best = jnp.maximum(best, jnp.max(wide, axis=1, keepdims=True))
+                factor = jnp.exp2(best - new_best)
+                weight, acc = weight * factor, acc * factor
+                wide = low
+                for i in range(per):
+                    if h + 1 < local_kv:
+                        wide = score(h + 1, u * per + i, i, wide)
+                    w = jnp.exp2(scores[h % 2, :, i * vid : (i + 1) * vid] - new_best)
+                    weight = weight + lanes(w, jnp.add)
+                    acc = acc + jnp.dot(
+                        w.astype(jnp.bfloat16), vbuf[u * per + i, :, h * HD : (h + 1) * HD],
+                        preferred_element_type=jnp.float32,
+                    )
+                done.append((new_best, weight, acc))
+            return tuple(done)
+
+        states = (
+            (
+                jnp.full((m_rows, 1), LOW, jnp.float32),
+                jnp.zeros((m_rows, HD), jnp.float32),
+                jnp.zeros((m_rows, HD), jnp.float32),
+            ),
+        ) * local_kv
         if n // per == 1:
-            state = part(0, state)
+            states = part(0, states)
         else:
-            state = lax.fori_loop(0, n // per, part, state)
-        _, weight, acc = state
-        total = jnp.maximum(jnp.sum(weight, axis=1, keepdims=True), 1.0)
-        result = jnp.where(seen > 0, acc / total, 0.0).astype(jnp.bfloat16)
-        for g in range(GROUP):
-            abuf[:, head_cols(h * GROUP + g)] = result[g * TBLK : (g + 1) * TBLK]
+            states = lax.fori_loop(0, n // per, part, states)
+        for h in range(local_kv):
+            _, weight, acc = states[h]
+            total = jnp.maximum(jnp.sum(weight, axis=1, keepdims=True), 1.0)
+            result = jnp.where(seen > 0, acc / total, 0.0).astype(jnp.bfloat16)
+            for g in range(GROUP):
+                head = h * GROUP + g
+                abuf[:, head * HD : (head + 1) * HD] = result[g * TBLK : (g + 1) * TBLK]
 
     def combine(c):
         wide = 512
@@ -328,11 +341,7 @@
 
         seen = visible_tokens(c)
 
-        def head(h, carry):
-            attend(c, h, seen)
-            return carry
-
-        lax.fori_loop(0, local_kv, head, 0)
+        attend(seen)
         guarded(c - p + 1 >= 0, sum_last, c - p + 1)
         for h in range(p - 2, 0, -1):
             guarded(c - h >= 0, sum_hop, c - h, h)
@@ -395,7 +404,7 @@
                 pltpu.VMEM((n,) + values.shape, bf16),
                 pltpu.VMEM((TBLK, q_cols), bf16),
                 pltpu.VMEM((TBLK, q_cols), bf16),
-                pltpu.VMEM((GROUP * TBLK, min(n * vid, max(vid, SUPER))), f32),
+                pltpu.VMEM((2, GROUP * TBLK, min(n * vid, max(vid, SUPER))), f32),
                 pltpu.VMEM((chunks * p, TBLK, out_cols), f32),
                 pltpu.VMEM((chunks * p, TBLK, out_cols), bf16),
                 pltpu.VMEM((chunks * p, TBLK, out_cols), bf16),

time: 78.1 us -> 76.9 us (0.985)
  Pallas kernels: 75.4 us -> 74.2 us
    pallas_call x1, Pallas kernels: 75.4 us -> 74.2 us  [shards(): pl.pallas_call(functools.partial(kernel, n, p), out_shape=jax.ShapeDtypeS...]
where the time goes in v2:
time: 76.9 us; the launch traced here: 76.7 us
  Pallas kernels  74.2 us (96%)
  local copies, waits for them, and re-layouts  1.87 us (2%)
    pallas_call x1, Pallas kernels, shards(): pl.pallas_call(functools.partial(kernel, n, p), out_shape=jax.ShapeDtypeS...  74.2 us
    unnamed x1, local copies, waits for them, and re-layouts  1.87 us

profile of v2, /device:TPU:1, one launch (start us, length us, event | category | flops | bytes accessed | tf_op | source)
XLA Modules:
  0.0 76.7 jit_solution(13960301891554876092)
XLA Ops:
  0.7 74.2 %shard_map.82 = bf16[256,1024]{1,0:T(8,128)(2,1)} custom-call(bf16[256,1024]{1,0:T(8,128)(2,1)} %text.1, bf16[4096,1024]{1,0:T(8,128)(2,1)} %wq_hbm.1, bf16[512,256]{1,0:T(8,128)(2,1)} %k_hbm.1, bf16[512,256]{1,0:T(8,128)(2,1)} %v_hbm.1, bf16[1024,4096]{1,0:T(8,128)(2,1)} %wo_hbm.1, f32[1]{0:T(128)S(6)} %copy.10.gate, s32[16]{0:T(128)} %lengths.1, s32[32]{0:T(128)} %limits.1), custom_call_target="tpu_custom_call" | custom-call | tf_op jit(solution)/shard_map/pallas_call | solution.py:394
  74.8 1.9 %copy.11 = bf16[256,1024]{1,0:T(8,128)(2,1)} copy(bf16[256,1024]{1,0:T(8,128)(2,1)} %shard_map.82) | data formatting | bytes 1048576
